TPU v7x, 32 devices: a whole 2x2x4 slice. The times are simulated.
32 devices in a mesh: dp: 8 (over z, x), vocab: 4 (over y, core).
Axes of the slice: x: 2, y: 2, z: 4, core: 2. Of those that a mesh axis runs over, the one named last changes fastest.
Arguments:
- hidden_states: bfloat16 [1024, 3584], P('dp', 'vocab'), may hold values from -750 to 750, as said below
- head_weight: bfloat16 [152064, 3584], P(('dp', 'vocab')), may hold values from -0.09375 to 0.09375
- token_ids: int32 [1024], P('dp'), may hold values from 0 to 152063
- response_mask: int32 [1024], P('dp'), may hold values 0 or 1
- rollout_logprobs: float32 [1024], P('dp'), may hold values from -14 to -6
- advantages: float32 [1024], P('dp'), may hold values from -6 to 6
Outputs:
- logprobs: float32 [1024], P('dp')
- tis_weight: float32 [1024], P('dp')
- loss: float32 [], replicated
Inputs may be any that keep to these rules, and one draw needn't show every extreme that they name: `hidden_states`: hidden states; some rows may be far larger than others.
All inputs are finite; a program needn't handle non-finite values. No bound on the sum of `response_mask` on one device may be relied on, other than what follows from the above.
Results may differ from a plain program's by a relative error of at most 0.0003.
Values may be sent and summed in bfloat16 or wider, within the bound.
A program may use at most 128 MiB of HBM per device.

v0:
```python
import jax
import jax.numpy as jnp
from jax import lax
from jax.sharding import PartitionSpec as P


def shard_stats(logits, ids_block, columns):
    matched = columns[None, :] == ids_block[:, None]
    picked = jnp.sum(jnp.where(matched, logits, 0.0), axis=1)
    peak = jnp.max(logits, axis=1)
    total = jnp.sum(jnp.exp(logits - peak[:, None]), axis=1)
    return (peak, total, picked)


def token_terms(logp, rollout, advant, mask):
    weight = jnp.minimum(jnp.exp(logp - rollout), 2.0)
    counted = mask.astype(jnp.float32)
    loss_part = -jnp.sum(counted * weight * advant * logp)
    return (weight, loss_part, jnp.sum(counted))


def body(hidden_states, head_weight, token_ids, response_mask, rollout_logprobs, advantages):
    rows_local = token_ids.shape[0]
    vocab_local = head_weight.shape[0]
    offset = lax.axis_index(("dp", "vocab")) * vocab_local
    own_columns = lax.iota(jnp.int32, vocab_local) + offset
    dp_index = lax.axis_index("dp")
    own_start = dp_index * rows_local
    all_ids, all_mask = (
        lax.all_gather(token_ids, "dp", axis=0, tiled=True),
        lax.all_gather(response_mask, "dp", axis=0, tiled=True),
    )
    all_rollout, all_advant = (
        lax.all_gather(rollout_logprobs, "dp", axis=0, tiled=True),
        lax.all_gather(advantages, "dp", axis=0, tiled=True),
    )
    full_rows = lax.all_gather(hidden_states, "vocab", axis=1, tiled=True)
    logits = jnp.einsum(
        "rd,vd->rv",
        lax.all_gather(full_rows, "dp", axis=0, tiled=True),
        head_weight,
        preferred_element_type=jnp.float32,
    )
    peak, total, picked = shard_stats(logits, all_ids, own_columns)
    peak, total, picked = (peak, total, picked)
    top = lax.pmax(peak, ("dp", "vocab"))
    total_sum, picked_sum = lax.psum((total * jnp.exp(peak - top), picked), ("dp", "vocab"))
    logprob_all = picked_sum - (top + jnp.log(total_sum))
    own_logp = lax.dynamic_slice_in_dim(logprob_all, own_start, rows_local, 0)
    weight_all, loss_sum, count = token_terms(logprob_all, all_rollout, all_advant, all_mask)
    weight = lax.dynamic_slice_in_dim(weight_all, own_start, rows_local, 0)
    loss = loss_sum / jnp.maximum(count, 1.0)
    return (own_logp, weight, loss)


def solution(mesh):
    placed = (P("dp", "vocab"), P(("dp", "vocab"), None), P("dp"), P("dp"), P("dp"), P("dp"))
    return jax.shard_map(
        body, mesh=mesh, in_specs=placed, out_specs=(P("dp"), P("dp"), P()), check_vma=False
    )
```

profile of v0, /device:TPU:0, one launch (start us, length us, event | category | flops | bytes accessed | tf_op | source)
XLA Modules:
  0.0 274.0 jit_solution(17611963197525337187)
XLA Ops:
  7.2 0.0 all-gather.6.cloned.1.call-start
  7.2 12.5 %all_gather.19 = bf16[128,3584]{1,0:T(8,128)(2,1)} all-gather(bf16[128,896]{1,0:T(8,128)(2,1)} %param.6), channel_id=1, replica_groups=mesh['dp'=8,'vocab'=4] {'vocab'}, dimensions={1}, use_global_device_ids=true | all-gather | bytes 1146880 | tf_op jit(solution)/shard_map/all_gather | solution.py:37
  19.7 0.0 all-gather.6.cloned.1.call-update
  19.7 21.4 %all-gather.2 = s32[8,1,128]{2,1,0:T(1,128)S(1)} all-gather(s32[1,1,128]{2,1,0:T(1,128)} %bitcast.15), channel_id=1, replica_groups=mesh['dp'=8,'vocab'=4] {'dp'}, dimensions={0}, use_global_device_ids=true | all-gather | bytes 4608 | tf_op jit(solution)/shard_map/all_gather | solution.py:31
  41.2 0.6 convert_reduce_fusion
  42.4 17.1 %all-gather = s32[8,1,128]{2,1,0:T(1,128)S(1)} all-gather(s32[1,1,128]{2,1,0:T(1,128)} %bitcast.16), channel_id=1, replica_groups=mesh['dp'=8,'vocab'=4] {'dp'}, dimensions={0}, use_global_device_ids=true | all-gather | bytes 4608 | tf_op jit(solution)/shard_map/all_gather | solution.py:30
  59.5 18.8 %all-gather.1 = f32[8,1,128]{2,1,0:T(1,128)S(1)} all-gather(f32[1,1,128]{2,1,0:T(1,128)} %bitcast.17), channel_id=1, replica_groups=mesh['dp'=8,'vocab'=4] {'dp'}, dimensions={0}, use_global_device_ids=true | all-gather | bytes 4608 | tf_op jit(solution)/shard_map/all_gather | solution.py:34
  78.3 17.3 %all-gather.3 = f32[8,1,128]{2,1,0:T(1,128)S(1)} all-gather(f32[1,1,128]{2,1,0:T(1,128)} %bitcast.18), channel_id=1, replica_groups=mesh['dp'=8,'vocab'=4] {'dp'}, dimensions={0}, use_global_device_ids=true | all-gather | bytes 4608 | tf_op jit(solution)/shard_map/all_gather | solution.py:35
  95.6 36.2 %all-gather.6.cloned.1.call-done = bf16[1024,3584]{1,0:T(8,128)(2,1)} async-done(((bf16[128,3584]{1,0:T(8,128)(2,1)}), bf16[1024,3584]{1,0:T(8,128)(2,1)}) %all-gather.6.cloned.1.call-update) | async-done | bytes 7340048 | tf_op jit(solution)/shard_map/all_gather | solution.py:40
  131.8 43.0 %fusion = (f32[1024]{0:T(1024)S(1)}, f32[1024,4752]{0,1:T(8,128)}) fusion(bf16[1024,3584]{1,0:T(8,128)(2,1)} %all-gather.6.cloned.1.call-done, bf16[4752,3584]{1,0:T(8,128)(2,1)} %param.7), kind=kOutput, calls=%fused_computation.8 | convolution fusion | flops 34884698112 | bytes 60870656 | tf_op jit(solution)/shard_map/rd,vd->rv/dot_general | solution.py:38
  174.8 38.4 %pmax.7 = f32[1024]{0:T(1024)S(1)} all-reduce(f32[1024]{0:T(1024)S(1)} %get-tuple-element.9), channel_id=1, replica_groups=mesh['dp'=8,'vocab'=4] {'dp','vocab'}, use_global_device_ids=true, to_apply=%region_3.4 | all-reduce | flops 1024 | bytes 8192 | tf_op jit(solution)/shard_map/pmax | solution.py:46
  213.1 9.5 %exponential_reduce_fusion = (f32[1024]{0:T(1024)S(1)}, f32[1024]{0:T(1024)S(1)}) fusion(f32[1024,4752]{0,1:T(8,128)} %get-tuple-element.10, f32[1024]{0:T(1024)S(1)} %get-tuple-element.9, s32[1024]{0:T(1024)S(1)} %bitcast.14, s32[4752]{0:T(1024)S(1)} %iota_add_fusion), kind=kLoop, calls=%fused_computation | loop fusion | flops 24328192 | bytes 19499584 | tf_op jit(solution)/shard_map/reduce_sum | solution.py:11
  222.7 40.8 %all-reduce = (f32[1024]{0:T(1024)S(1)}, f32[1024]{0:T(1024)S(1)}) all-reduce(f32[1024]{0:T(1024)S(1)} %get-tuple-element.4, f32[1024]{0:T(1024)S(1)} %exponential_multiply_fusion), channel_id=1, replica_groups=mesh['dp'=8,'vocab'=4] {'dp','vocab'}, use_global_device_ids=true, to_apply=%region_1.2 | all-reduce | flops 2048 | bytes 16384 | tf_op jit(solution)/shard_map/psum | solution.py:47
  263.5 0.6 multiply_reduce_fusion
  264.1 0.6 dynamic_slice.6
  264.7 0.6 dynamic_slice.7
  (4 shorter events, 0.0 us)
Async XLA Ops:
  7.2 124.6 %all-gather.6.cloned.1.call-start = ((), (), s32[]{:S(2)}) async-start(), calls=%async_computation | async-start | bytes 8257536 | tf_op jit(solution)/shard_map/all_gather | solution.py:40
Sparse Core Ops, SparseCore 0:
  19.8 111.9 all-gather.5
where the time goes:
time: 275 us; the launch traced here: 274 us
  blocking collectives  166 us (60%)
  matrix products  43 us (16%)
  waiting for transfers between devices  36.2 us (13%)
  between operations  16.5 us (6%)
  other arithmetic  10.8 us (4%)
    dot_general x1, matrix products, body(): jnp.einsum('rd,vd->rv', lax.all_gather(full_rows, 'dp', axis=0, tiled=Tru...  43 us
    psum x1, blocking collectives, body(): lax.psum((total * jnp.exp(peak - top), picked), ('dp', 'vocab'))  40.8 us
    pmax x1, blocking collectives, body(): top = lax.pmax(peak, ('dp', 'vocab'))  38.4 us
    all_gather x1, waiting for transfers between devices, body(): lax.all_gather(full_rows, 'dp', axis=0, tiled=True)  36.2 us
    all_gather x1, blocking collectives, body(): lax.all_gather(response_mask, 'dp', axis=0, tiled=True)  21.4 us
    all_gather x1, blocking collectives, body(): lax.all_gather(rollout_logprobs, 'dp', axis=0, tiled=True)  18.8 us
    all_gather x1, blocking collectives, body(): lax.all_gather(advantages, 'dp', axis=0, tiled=True)  17.3 us
    all_gather x1, blocking collectives, body(): lax.all_gather(token_ids, 'dp', axis=0, tiled=True)  17.1 us
  transfers between devices with their start and end apart: 1, of which 1 were waited for; matrix products, arithmetic and copies ran while one was open for 0% of the time, Pallas kernels for 0%

commit v1 on v0

--- a/solution.py
+++ b/solution.py
@@ -2,6 +2,11 @@
 import jax.numpy as jnp
 from jax import lax
 from jax.sharding import PartitionSpec as P
+
+
+def by_each_axis(x, one, other):
+    half = lax.psum(x, one)
+    return lax.psum(half, other)
 
 
 def shard_stats(logits, ids_block, columns):
@@ -44,7 +49,7 @@
     peak, total, picked = shard_stats(logits, all_ids, own_columns)
     peak, total, picked = (peak, total, picked)
     top = lax.pmax(peak, ("dp", "vocab"))
-    total_sum, picked_sum = lax.psum((total * jnp.exp(peak - top), picked), ("dp", "vocab"))
+    total_sum, picked_sum = by_each_axis((total * jnp.exp(peak - top), picked), "dp", "vocab")
     logprob_all = picked_sum - (top + jnp.log(total_sum))
     own_logp = lax.dynamic_slice_in_dim(logprob_all, own_start, rows_local, 0)
     weight_all, loss_sum, count = token_terms(logprob_all, all_rollout, all_advant, all_mask)

time: 275 us -> 261 us (0.949)
  blocking collectives: 166 us -> 153 us
    psum x1 -> x2, blocking collectives: 40.8 us -> 27.1 us  [the longest x1 21.4 us: by_each_axis(): half = lax.psum(x, one)]
where the time goes in v1:
time: 261 us; the launch traced here: 260 us
  blocking collectives  153 us (59%)
  matrix products  43 us (16%)
  waiting for transfers between devices  36.2 us (14%)
  between operations  16.5 us (6%)
  other arithmetic  10.8 us (4%)
    dot_general x1, matrix products, body(): jnp.einsum('rd,vd->rv', lax.all_gather(full_rows, 'dp', axis=0, tiled=Tru...  43 us
    pmax x1, blocking collectives, body(): top = lax.pmax(peak, ('dp', 'vocab'))  38.3 us
    all_gather x1, waiting for transfers between devices, body(): lax.all_gather(full_rows, 'dp', axis=0, tiled=True)  36.2 us
    all_gather x1, blocking collectives, body(): lax.all_gather(response_mask, 'dp', axis=0, tiled=True)  21.4 us
    psum x1, blocking collectives, by_each_axis(): half = lax.psum(x, one)  21.4 us
    all_gather x1, blocking collectives, body(): lax.all_gather(rollout_logprobs, 'dp', axis=0, tiled=True)  18.8 us
    all_gather x1, blocking collectives, body(): lax.all_gather(advantages, 'dp', axis=0, tiled=True)  17.3 us
    all_gather x1, blocking collectives, body(): lax.all_gather(token_ids, 'dp', axis=0, tiled=True)  17.1 us
  transfers between devices with their start and end apart: 1, of which 1 were waited for; matrix products, arithmetic and copies ran while one was open for 0% of the time, Pallas kernels for 0%

profile of v1, /device:TPU:0, one launch (start us, length us, event | category | flops | bytes accessed | tf_op | source)
XLA Modules:
  0.0 260.3 jit_solution(3381287871608712470)
XLA Ops:
  7.2 0.0 all-gather.6.cloned.1.call-start
  7.2 12.5 %all_gather.19 = bf16[128,3584]{1,0:T(8,128)(2,1)} all-gather(bf16[128,896]{1,0:T(8,128)(2,1)} %param.6), channel_id=1, replica_groups=mesh['dp'=8,'vocab'=4] {'vocab'}, dimensions={1}, use_global_device_ids=true | all-gather | bytes 1146880 | tf_op jit(solution)/shard_map/all_gather | solution.py:42
  19.7 0.0 all-gather.6.cloned.1.call-update
  19.7 21.4 %all-gather.2 = s32[8,1,128]{2,1,0:T(1,128)S(1)} all-gather(s32[1,1,128]{2,1,0:T(1,128)} %bitcast.15), channel_id=1, replica_groups=mesh['dp'=8,'vocab'=4] {'dp'}, dimensions={0}, use_global_device_ids=true | all-gather | bytes 4608 | tf_op jit(solution)/shard_map/all_gather | solution.py:36
  41.2 0.6 convert_reduce_fusion
  42.4 17.1 %all-gather = s32[8,1,128]{2,1,0:T(1,128)S(1)} all-gather(s32[1,1,128]{2,1,0:T(1,128)} %bitcast.16), channel_id=1, replica_groups=mesh['dp'=8,'vocab'=4] {'dp'}, dimensions={0}, use_global_device_ids=true | all-gather | bytes 4608 | tf_op jit(solution)/shard_map/all_gather | solution.py:35
  59.5 18.8 %all-gather.1 = f32[8,1,128]{2,1,0:T(1,128)S(1)} all-gather(f32[1,1,128]{2,1,0:T(1,128)} %bitcast.17), channel_id=1, replica_groups=mesh['dp'=8,'vocab'=4] {'dp'}, dimensions={0}, use_global_device_ids=true | all-gather | bytes 4608 | tf_op jit(solution)/shard_map/all_gather | solution.py:39
  78.3 17.3 %all-gather.3 = f32[8,1,128]{2,1,0:T(1,128)S(1)} all-gather(f32[1,1,128]{2,1,0:T(1,128)} %bitcast.18), channel_id=1, replica_groups=mesh['dp'=8,'vocab'=4] {'dp'}, dimensions={0}, use_global_device_ids=true | all-gather | bytes 4608 | tf_op jit(solution)/shard_map/all_gather | solution.py:40
  95.6 36.2 %all-gather.6.cloned.1.call-done = bf16[1024,3584]{1,0:T(8,128)(2,1)} async-done(((bf16[128,3584]{1,0:T(8,128)(2,1)}), bf16[1024,3584]{1,0:T(8,128)(2,1)}) %all-gather.6.cloned.1.call-update) | async-done | bytes 7340048 | tf_op jit(solution)/shard_map/all_gather | solution.py:45
  131.8 43.0 %fusion = (f32[1024]{0:T(1024)S(1)}, f32[1024,4752]{0,1:T(8,128)}) fusion(bf16[1024,3584]{1,0:T(8,128)(2,1)} %all-gather.6.cloned.1.call-done, bf16[4752,3584]{1,0:T(8,128)(2,1)} %param.7), kind=kOutput, calls=%fused_computation.8 | convolution fusion | flops 34884698112 | bytes 60870656 | tf_op jit(solution)/shard_map/rd,vd->rv/dot_general | solution.py:43
  174.8 38.3 %pmax.7 = f32[1024]{0:T(1024)S(1)} all-reduce(f32[1024]{0:T(1024)S(1)} %get-tuple-element.11), channel_id=1, replica_groups=mesh['dp'=8,'vocab'=4] {'dp','vocab'}, use_global_device_ids=true, to_apply=%region_4.5 | all-reduce | flops 1024 | bytes 8192 | tf_op jit(solution)/shard_map/pmax | solution.py:51
  213.1 9.5 %exponential_reduce_fusion = (f32[1024]{0:T(1024)S(1)}, f32[1024]{0:T(1024)S(1)}) fusion(f32[1024,4752]{0,1:T(8,128)} %get-tuple-element.12, f32[1024]{0:T(1024)S(1)} %get-tuple-element.11, s32[1024]{0:T(1024)S(1)} %bitcast.14, s32[4752]{0:T(1024)S(1)} %iota_add_fusion), kind=kLoop, calls=%fused_computation | loop fusion | flops 24328192 | bytes 19499584 | tf_op jit(solution)/shard_map/reduce_sum | solution.py:16
  222.7 21.4 %all-reduce = (f32[1024]{0:T(1024)S(1)}, f32[1024]{0:T(1024)S(1)}) all-reduce(f32[1024]{0:T(1024)S(1)} %get-tuple-element.4, f32[1024]{0:T(1024)S(1)} %exponential_multiply_fusion), channel_id=1, replica_groups=mesh['dp'=8,'vocab'=4] {'dp'}, use_global_device_ids=true, to_apply=%region_1.2 | all-reduce | flops 2048 | bytes 16384 | tf_op jit(solution)/shard_map/psum | solution.py:8
  244.0 5.8 %all-reduce.1 = (f32[1024]{0:T(1024)S(1)}, f32[1024]{0:T(1024)S(1)}) all-reduce(f32[1024]{0:T(1024)S(1)} %get-tuple-element.5, f32[1024]{0:T(1024)S(1)} %get-tuple-element.6), channel_id=1, replica_groups=mesh['dp'=8,'vocab'=4] {'vocab'}, use_global_device_ids=true, to_apply=%region_2.3 | all-reduce | flops 2048 | bytes 16384 | tf_op jit(solution)/shard_map/psum | solution.py:9
  249.8 0.6 multiply_reduce_fusion
  250.4 0.6 dynamic_slice.6
  251.0 0.6 dynamic_slice.7
  (4 shorter events, 0.0 us)
Async XLA Ops:
  7.2 124.6 %all-gather.6.cloned.1.call-start = ((), (), s32[]{:S(2)}) async-start(), calls=%async_computation | async-start | bytes 8257536 | tf_op jit(solution)/shard_map/all_gather | solution.py:45
Sparse Core Ops, SparseCore 0:
  19.8 111.9 all-gather.5
